TPU v7x, 32 devices: a whole 2x2x4 slice. The times are simulated.
32 devices in a mesh: freq: 4 (over y, x), pts: 8 (over z, core).
Axes of the slice: x: 2, y: 2, z: 4, core: 2. Of those that a mesh axis runs over, the one named last changes fastest.
Arguments:
- data: float32 [2, 32, 64, 3, 8192], P(None, 'freq', None, None, 'pts'), may hold values from -180 to 180
- quad_weight: float32 [8192], P('pts'), may hold values from 0.2 to 5
- basis: float32 [2, 32, 64, 8], P(None, 'freq'), may hold values from -6 to 6
Outputs:
- basis_out: float32 [2, 32, 64, 8], P(None, 'freq')
- spectrum: float32 [32, 8], P('freq')
- modes: float32 [2, 32, 8, 3, 8192], P(None, 'freq', None, None, 'pts')
All inputs are finite; a program needn't handle non-finite values.
Results may differ from a plain program's by a relative error of at most 0.0001.
Values sent between devices are 32-bit elements; how exact they have to be, the bound alone decides.
A program may use at most 128 MiB of HBM per device.

v0:
```python
import functools

import jax
import jax.numpy as jnp
from jax import lax
from jax.experimental import pallas as pl
from jax.experimental.pallas import tpu as pltpu
from jax.sharding import PartitionSpec as P

ITERS = 4
MESH = pl.DeviceIdType.MESH


def spod_kernel(
    scaling,
    freqs,
    peers,
    groups,
    data_ref,
    weight_hbm,
    basis_hbm,
    split,
    message_ref,
    inverse_ref,
    buf,
    weight_ref,
    basis_ref,
    small_sem,
    gram_out,
    gram_in,
    trace_out,
    trace_in,
    message,
    load_sem,
    gram_send,
    gram_recv,
    trace_send,
    trace_recv,
    msg_send,
    msg_recv,
):
    comps, blocks, points = buf.shape[2], buf.shape[3], buf.shape[4]
    rank = basis_ref.shape[1]
    wide = 2 * blocks
    stride = peers // freqs
    me = lax.axis_index("pts")
    row = lax.axis_index("freq")
    mine = me // stride
    is_owner = lax.rem(me, stride) == 0

    def load(f):
        return pltpu.make_async_copy(data_ref.at[:, f], buf.at[f], load_sem.at[f])

    def order(i):
        return lax.rem(mine + 1 + i, freqs)

    weight_load = pltpu.make_async_copy(weight_hbm, weight_ref, small_sem.at[0])
    basis_load = pltpu.make_async_copy(basis_hbm.at[:, mine], basis_ref, small_sem.at[1])
    weight_load.start()
    for i in range(freqs):
        load(order(i)).start()
    basis_load.start()

    barrier = pltpu.get_barrier_semaphore()
    for step in range(1, peers):
        pl.semaphore_signal(
            barrier, inc=1, device_id={"pts": lax.rem(me + step, peers)}, device_id_type=MESH
        )
    for step in range(1, groups):
        pl.semaphore_signal(
            barrier, inc=1, device_id={"freq": lax.rem(row + step, groups)}, device_id_type=MESH
        )

    weight_load.wait()
    root = jnp.sqrt(weight_ref[...])
    inverse_ref[...] = (1.0 / blocks) / root
    lanes = lax.broadcasted_iota(jnp.int32, (1, wide), 1)
    low_minus = jnp.where(lanes < blocks, -1.0, 1.0).astype(jnp.float32)
    high_minus = -low_minus

    def local_gram(f):
        load(f).wait()
        total = jnp.zeros((wide, 2 * wide), jnp.float32)
        for c in range(comps):
            for part in range(2):
                value = buf[f, part, c] * root
                high = value.astype(jnp.bfloat16)
                rest = (value - high.astype(jnp.float32)).astype(jnp.bfloat16)
                split[f, c, part * blocks : (part + 1) * blocks] = high
                split[f, c, wide + part * blocks : wide + (part + 1) * blocks] = rest
            total = total + lax.dot_general(
                split[f, c, :wide],
                split[f, c],
                (((1,), (1,)), ((), ())),
                preferred_element_type=jnp.float32,
            )
        half = 0.5 * total[:, :wide] + total[:, wide:]
        return half[:blocks] + high_minus * pltpu.roll(half[blocks:], blocks, 1)

    def gram_copy(f):
        return pltpu.make_async_remote_copy(
            src_ref=gram_out.at[f],
            dst_ref=gram_in.at[me],
            send_sem=gram_send.at[f],
            recv_sem=gram_recv.at[me],
            device_id={"pts": f * stride},
            device_id_type=MESH,
        )

    first = order(0)
    gram_out[first] = local_gram(first)
    pl.semaphore_wait(barrier, peers - 1 + groups - 1)
    gram_copy(first).start()

    def middle(i, carry):
        f = order(i)
        gram_out[f] = local_gram(f)
        gram_copy(f).start()
        return carry

    lax.fori_loop(1, freqs - 1, middle, 0)
    gram_out[mine] = local_gram(mine)

    if stride > 1:

        @pl.when(jnp.logical_not(is_owner))
        def _():
            gram_copy(mine).start()

    def trace_copy(step):
        return pltpu.make_async_remote_copy(
            src_ref=trace_out,
            dst_ref=trace_in.at[row],
            send_sem=trace_send.at[step],
            recv_sem=trace_recv.at[row],
            device_id={"freq": lax.rem(row + step, groups)},
            device_id_type=MESH,
        )

    def msg_copy(step):
        return pltpu.make_async_remote_copy(
            src_ref=message.at[mine],
            dst_ref=message.at[mine],
            send_sem=msg_send.at[step],
            recv_sem=msg_recv.at[mine],
            device_id={"pts": lax.rem(me + step, peers)},
            device_id_type=MESH,
        )

    basis_load.wait()

    @pl.when(is_owner)
    def _():
        def gather(step, total):
            source = lax.rem(me + step, peers)
            pltpu.make_async_copy(gram_in.at[source], gram_in.at[source], gram_recv.at[source]).wait()
            return total + gram_in[source]

        total = lax.fori_loop(1, peers, gather, gram_out[mine]) * scaling
        double = jnp.concatenate([high_minus * total, pltpu.roll(total, blocks, 1)], axis=0)
        matrix = double + double.T
        rows_at = lax.broadcasted_iota(jnp.int32, (wide, wide), 0)
        cols_at = lax.broadcasted_iota(jnp.int32, (wide, wide), 1)
        diagonal = jnp.where(rows_at == cols_at, matrix, 0.0)
        trace = 0.5 * jnp.sum(jnp.sum(diagonal, axis=0, keepdims=True), axis=1, keepdims=True)
        trace_out[...] = jnp.broadcast_to(trace, trace_out.shape)
        for step in range(1, groups):
            trace_copy(step).start()

        def apply(vec):
            return jnp.dot(
                vec, matrix, precision=lax.Precision.HIGHEST, preferred_element_type=jnp.float32
            )

        which = lax.broadcasted_iota(jnp.int32, (rank, wide), 0)

        def step_body(step, vec):
            z = apply(vec)
            turned = low_minus * pltpu.roll(z, blocks, 1)
            for j in range(rank):
                base = z[j : j + 1]
                base_turned = turned[j : j + 1]
                along = jnp.sum(z * base, axis=1, keepdims=True) * (1.0 / blocks)
                across = jnp.sum(z * base_turned, axis=1, keepdims=True) * (1.0 / blocks)
                factor = lax.rsqrt(along[j : j + 1] + 1e-06)
                unit = base * factor
                unit_turned = base_turned * factor
                along = along * factor
                across = across * factor
                z_next = z - (along * unit + across * unit_turned)
                turned_next = turned - (along * unit_turned - across * unit)
                z = jnp.where(which > j, z_next, jnp.where(which == j, unit, z))
                turned = jnp.where(which > j, turned_next, turned)
            return z

        start = jnp.concatenate([basis_ref[0], basis_ref[1]], axis=1)
        vec = lax.fori_loop(0, ITERS, step_body, start)
        energy = jnp.sum(vec * apply(vec), axis=1, keepdims=True) * (1.0 / blocks)
        columns = lax.broadcasted_iota(jnp.int32, (rank, wide), 1)
        energy_row = jnp.sum(jnp.where(which == columns, energy, 0.0), axis=0, keepdims=True)

        group_trace = trace_out[...]
        for step in range(1, groups):
            source = lax.rem(row + step, groups)
            pltpu.make_async_copy(trace_in.at[source], trace_in.at[source], trace_recv.at[source]).wait()
            group_trace = group_trace + trace_in[source]
        message[mine, 0:rank] = vec
        message[mine, rank : rank + 8] = jnp.where(
            lax.broadcasted_iota(jnp.int32, (8, wide), 0) == 0, energy_row, group_trace
        )
        for step in range(1, peers):
            msg_copy(step).start()

    def arrive(f):
        pltpu.make_async_copy(message.at[f], message.at[f], msg_recv.at[f]).wait()

    if stride > 1:

        @pl.when(jnp.logical_not(is_owner))
        def _():
            arrive(mine)

    def others(i, carry):
        arrive(lax.rem(mine + i, freqs))
        return carry

    lax.fori_loop(1, freqs, others, 0)
    message_ref[...] = message[...]

    def finish(i, carry):
        gram_copy(order(i)).wait_send()
        return carry

    lax.fori_loop(0, freqs - 1, finish, 0)
    if stride > 1:

        @pl.when(jnp.logical_not(is_owner))
        def _():
            gram_copy(mine).wait_send()

    @pl.when(is_owner)
    def _():
        for step in range(1, groups):
            trace_copy(step).wait_send()
        for step in range(1, peers):
            msg_copy(step).wait_send()


def project_kernel(
    count, inverse_ref, split, message, basis_out_ref, spectrum_ref, modes_ref, stage, store_sem
):
    freqs, comps, depth, points = split.shape
    wide = depth // 2
    blocks = wide // 2
    rank = spectrum_ref.shape[1]
    inverse = inverse_ref[...]
    lanes = lax.broadcasted_iota(jnp.int32, (1, wide), 1)
    high_minus = jnp.where(lanes < blocks, 1.0, -1.0).astype(jnp.float32)

    def store(f):
        return pltpu.make_async_copy(stage.at[f], modes_ref.at[:, f], store_sem.at[f])

    def project(f, carry):
        vec = message[f, 0:rank]
        left = jnp.concatenate([high_minus * vec, pltpu.roll(vec, blocks, 1)], axis=0)
        high = left.astype(jnp.bfloat16)
        rest = (left - high.astype(jnp.float32)).astype(jnp.bfloat16)
        both = jnp.concatenate([high, high], axis=1)
        tail = jnp.concatenate([rest, jnp.zeros_like(rest)], axis=1)
        left = jnp.concatenate([both, tail], axis=0)
        for c in range(comps):
            out = jnp.dot(left, split[f, c], preferred_element_type=jnp.float32)
            out = (out[: 2 * rank] + out[2 * rank :]) * inverse
            stage[f, 0, c] = out[:rank]
            stage[f, 1, c] = out[rank:]
        store(f).start()
        basis_out_ref[0, f] = vec[:, :blocks]
        basis_out_ref[1, f] = pltpu.roll(vec, blocks, 1)[:, :blocks]
        return carry

    lax.fori_loop(0, freqs, project, 0, unroll=True)

    energies = []
    overall = jnp.zeros((1, wide), jnp.float32)
    for f in range(freqs):
        energies.append(message[f, rank : rank + 1])
        overall = overall + message[f, rank + 1 : rank + 2]
    spectrum_ref[...] = (jnp.concatenate(energies, axis=0) * count / overall)[:, :rank]
    for f in range(freqs):
        store(f).wait()


def per_device(peers, groups, data, quad_weight, basis):
    _, freqs, blocks, comps, points = data.shape
    rank = basis.shape[-1]
    assert peers % freqs == 0 and freqs > 2
    scaling = 1.0 / (comps * points * peers)
    wide = 2 * blocks
    vmem = pl.BlockSpec(memory_space=pltpu.VMEM)
    anywhere = pl.BlockSpec(memory_space=pl.ANY)
    f32 = jnp.float32
    weight = quad_weight.reshape(1, points)
    hbm = pl.BlockSpec(memory_space=pltpu.HBM)
    in_hbm = functools.partial(pltpu.with_memory_space_constraint, memory_space=pltpu.HBM)
    split, message, inverse = pl.pallas_call(
        functools.partial(spod_kernel, scaling, freqs, peers, groups),
        out_shape=(
            pltpu.VMEM((freqs, comps, 2 * wide, points), jnp.bfloat16),
            pltpu.VMEM((freqs, rank + 8, wide), f32),
            pltpu.VMEM((1, points), f32),
        ),
        in_specs=[hbm, hbm, hbm],
        out_specs=(vmem, vmem, vmem),
        scratch_shapes=[
            pltpu.VMEM((freqs, 2, comps, blocks, points), f32),
            pltpu.VMEM((1, points), f32),
            pltpu.VMEM((2, rank, blocks), f32),
            pltpu.SemaphoreType.DMA((2,)),
            pltpu.VMEM((freqs, blocks, wide), f32),
            pltpu.VMEM((peers, blocks, wide), f32),
            pltpu.VMEM((8, wide), f32),
            pltpu.VMEM((groups, 8, wide), f32),
            pltpu.VMEM((freqs, rank + 8, wide), f32),
            pltpu.SemaphoreType.DMA((freqs,)),
            pltpu.SemaphoreType.DMA((freqs,)),
            pltpu.SemaphoreType.DMA((peers,)),
            pltpu.SemaphoreType.DMA((groups,)),
            pltpu.SemaphoreType.DMA((groups,)),
            pltpu.SemaphoreType.DMA((peers,)),
            pltpu.SemaphoreType.DMA((freqs,)),
        ],
        compiler_params=pltpu.CompilerParams(
            collective_id=0, has_side_effects=True, vmem_limit_bytes=40 * 1024 * 1024
        ),
        name="spod",
    )(
        in_hbm(data.transpose(0, 1, 3, 2, 4)),
        in_hbm(weight),
        in_hbm(basis.transpose(0, 1, 3, 2)),
    )
    basis_t, spectrum, modes_t = pl.pallas_call(
        functools.partial(project_kernel, freqs * groups * blocks),
        out_shape=(
            jax.ShapeDtypeStruct((2, freqs, rank, blocks), f32),
            jax.ShapeDtypeStruct((freqs, rank), f32),
            jax.ShapeDtypeStruct((2, freqs, comps, rank, points), f32),
        ),
        in_specs=[vmem, vmem, vmem],
        out_specs=(vmem, vmem, anywhere),
        scratch_shapes=[
            pltpu.VMEM((freqs, 2, comps, rank, points), f32),
            pltpu.SemaphoreType.DMA((freqs,)),
        ],
        compiler_params=pltpu.CompilerParams(vmem_limit_bytes=20 * 1024 * 1024),
        name="project",
    )(inverse, split, message)
    return (
        basis_t.transpose(0, 1, 3, 2),
        spectrum,
        modes_t.transpose(0, 1, 3, 2, 4),
    )


def solution(mesh):
    in_specs = (P(None, "freq", None, None, "pts"), P("pts"), P(None, "freq", None, None))
    out_specs = (P(None, "freq", None, None), P("freq", None), P(None, "freq", None, None, "pts"))
    body = functools.partial(per_device, mesh.shape["pts"], mesh.shape["freq"])
    return jax.shard_map(
        body, mesh=mesh, in_specs=in_specs, out_specs=out_specs, check_vma=False
    )
```

profile of v0, /device:TPU:0, one launch (start us, length us, event | category | flops | bytes accessed | tf_op | source)
XLA Modules:
  0.0 25.6 jit_solution(628831612438620626)
XLA Ops:
  0.6 21.3 %spod.1 = (bf16[8,3,256,1024]{3,2,1,0:T(8,128)(2,1)S(1)}, f32[8,16,128]{2,1,0:T(8,128)S(1)}, f32[1,1024]{1,0:T(1,128)S(1)}) custom-call(f32[2,8,3,64,1024]{4,3,2,1,0:T(8,128)} %bitcast.5, f32[1,1024]{1,0:T(1,128)} %bitcast.7, f32[2,8,8,64]{3,2,1,0:T(8,128)} %bitcast.6), custom_call_target="tpu_custom_call" | custom-call | tf_op jit(solution)/shard_map/spod/pallas_call | solution.py:305
  22.0 3.7 %project.1 = (f32[2,8,8,64]{3,2,1,0:T(8,128)}, f32[8,8]{1,0:T(8,128)}, f32[2,8,3,8,1024]{4,3,2,1,0:T(8,128)}) custom-call(f32[1,1024]{1,0:T(1,128)S(1)} %get-tuple-element.9.inverse_ref, bf16[8,3,256,1024]{3,2,1,0:T(8,128)(2,1)S(1)} %get-tuple-element.10.split, f32[8,16,128]{2,1,0:T(8,128)S(1)} %get-tuple-element.11.message), custom_call_target="tpu_custom_call" | custom-call | tf_op jit(solution)/shard_map/project/pallas_call | solution.py:341
where the time goes:
time: 25.8 us; the launch traced here: 25.6 us
  Pallas kernels  25 us (97%)
  between operations  0.64 us (2%)
    pallas_call x1, Pallas kernels, per_device(): pl.pallas_call(functools.partial(spod_kernel, scaling, freqs, peers, grou...  21.3 us
    pallas_call x1, Pallas kernels, per_device(): pl.pallas_call(functools.partial(project_kernel, freqs * groups * blocks)...  3.66 us

commit v1 on v0

v1 whole, which is shorter than its diff:
```python
import functools

import jax
import jax.numpy as jnp
from jax import lax
from jax.experimental import pallas as pl
from jax.experimental.pallas import tpu as pltpu
from jax.sharding import PartitionSpec as P

ITERS = 4
EPS = 1e-06
MESH = pl.DeviceIdType.MESH


def partner(index, mask, size):
    if size & (size - 1):
        return lax.rem(index + mask, size)
    result, bit = 0, 1
    while bit < size:
        if isinstance(mask, int):
            one = lax.rem(lax.div(index, bit), 2)
            result = result + bit * (1 - one if mask & bit else one)
        else:
            one = lax.rem(lax.div(index, bit), 2)
            other = lax.rem(lax.div(mask, bit), 2)
            result = result + bit * (one + other - 2 * one * other)
        bit *= 2
    return result


def slot_of(source, target, size):
    return lax.rem(source - target - 1 + size, size)


def wait_bytes(ref, sem):
    pltpu.make_async_copy(ref, ref, sem).wait()


def project_one(vec, split, f, inverse, stage, at):
    rank, wide = vec.shape
    blocks = wide // 2
    lanes = lax.broadcasted_iota(jnp.int32, (1, wide), 1)
    high_minus = jnp.where(lanes < blocks, 1.0, -1.0).astype(jnp.float32)
    left = jnp.concatenate([high_minus * vec, pltpu.roll(vec, blocks, 1)], axis=0)
    high = left.astype(jnp.bfloat16)
    rest = (left - high.astype(jnp.float32)).astype(jnp.bfloat16)
    both = jnp.concatenate([high, high], axis=1)
    tail = jnp.concatenate([rest, jnp.zeros_like(rest)], axis=1)
    left = jnp.concatenate([both, tail], axis=0)
    for c in range(split.shape[1]):
        out = jnp.dot(left, split[f, c], preferred_element_type=jnp.float32)
        out = (out[: 2 * rank] + out[2 * rank :]) * inverse
        stage[at, 0, c] = out[:rank]
        stage[at, 1, c] = out[rank:]


def orthonormalize(z, turned, blocks, group):
    rank, wide = z.shape
    which = lax.broadcasted_iota(jnp.int32, (rank, wide), 0)
    for first in range(0, rank, group):
        rows = range(first, min(first + group, rank))
        real, imag = {}, {}
        for j in rows:
            real[j] = jnp.sum(z * z[j : j + 1], axis=1, keepdims=True)
            imag[j] = jnp.sum(z * turned[j : j + 1], axis=1, keepdims=True)
        for j in rows:
            real[j] = jnp.broadcast_to(real[j], z.shape) * (1.0 / blocks)
            imag[j] = jnp.broadcast_to(imag[j], z.shape) * (1.0 / blocks)
        for j in rows:
            square = jnp.maximum(real[j][j : j + 1], 0.0)
            factor = lax.rsqrt(square + EPS)
            gain = factor * factor
            gain = gain * (1.0 + EPS * gain)
            later = which > j
            along = jnp.where(later, real[j], 0.0)
            across = jnp.where(later, imag[j], 0.0)
            for k in rows:
                if k > j:
                    up = along[k : k + 1] * gain
                    side = across[k : k + 1] * gain
                    real[k] = real[k] - (up * along + side * across)
                    imag[k] = imag[k] - (up * across - side * along)
            unit = z[j : j + 1] * factor
            unit_turned = turned[j : j + 1] * factor
            along = along * factor
            across = across * factor
            z_next = z - (along * unit + across * unit_turned)
            turned = turned - (along * unit_turned - across * unit)
            z = jnp.where(which == j, unit, z_next)
    return z


def spod_kernel(
    scaling,
    freqs,
    peers,
    groups,
    early,
    data_ref,
    weight_hbm,
    basis_hbm,
    split,
    message_ref,
    scalar_ref,
    inverse_ref,
    stage,
    buf,
    weight_ref,
    basis_ref,
    raw,
    gram_out,
    gram_in,
    trace_out,
    trace_in,
    message,
    scalar_out,
    scalar_in,
    small_sem,
    load_sem,
    gram_sem,
    trace_sem,
    msg_send,
    msg_recv,
    scalar_sem,
):
    comps, blocks, points = buf.shape[2], buf.shape[3], buf.shape[4]
    rank = basis_ref.shape[1]
    wide = 2 * blocks
    half_rows = blocks // 2
    stride = peers // freqs
    me = lax.axis_index("pts")
    row = lax.axis_index("freq")
    mine = lax.div(me, stride)
    is_owner = lax.rem(me, stride) == 0
    hold = min(2, freqs - 1)
    f32 = jnp.float32

    def load(f):
        return pltpu.make_async_copy(data_ref.at[:, f], buf.at[f], load_sem.at[f])

    def order(i):
        return partner(mine, freqs - 1 - i, freqs)

    weight_load = pltpu.make_async_copy(weight_hbm, weight_ref, small_sem.at[0])
    basis_load = pltpu.make_async_copy(basis_hbm.at[:, mine], basis_ref, small_sem.at[1])
    weight_load.start()
    for i in range(freqs):
        load(order(i)).start()
    basis_load.start()

    barrier = pltpu.get_barrier_semaphore()
    for step in range(1, peers):
        pl.semaphore_signal(
            barrier, inc=1, device_id={"pts": lax.rem(me + step, peers)}, device_id_type=MESH
        )
    for step in range(1, groups):
        pl.semaphore_signal(
            barrier, inc=1, device_id={"freq": lax.rem(row + step, groups)}, device_id_type=MESH
        )

    lanes = lax.broadcasted_iota(jnp.int32, (1, wide), 1)
    low = lanes < blocks
    high_minus = jnp.where(low, 1.0, -1.0).astype(f32)
    raw[...] = jnp.zeros_like(raw)
    weight_load.wait()
    root = jnp.sqrt(weight_ref[...])
    inverse_ref[...] = (1.0 / blocks) / root

    rows_at = lax.broadcasted_iota(jnp.int32, (half_rows, wide), 0)
    cols_at = lax.broadcasted_iota(jnp.int32, (half_rows, wide), 1)
    diagonal = jnp.logical_or(cols_at == rows_at, cols_at == rows_at + blocks + half_rows)

    def local_gram(f):
        load(f).wait()
        total = jnp.zeros((2 * wide, wide), f32)
        for c in range(comps):
            for part in range(2):
                value = buf[f, part, c] * root
                high = value.astype(jnp.bfloat16)
                rest = (value - high.astype(f32)).astype(jnp.bfloat16)
                split[f, c, part * blocks : (part + 1) * blocks] = high
                split[f, c, wide + part * blocks : wide + (part + 1) * blocks] = rest
            total = total + lax.dot_general(
                split[f, c],
                split[f, c, :wide],
                (((1,), (1,)), ((), ())),
                preferred_element_type=f32,
            )
        raw[...] = 0.5 * total[:wide] + total[wide:]

    def pack(f):
        total = raw[...]
        both = total[:blocks] + high_minus * pltpu.roll(total[blocks:], blocks, 1)
        other = pltpu.roll(both, blocks, 1)
        minus = both - other
        flipped = jnp.concatenate([minus, minus], axis=0).T
        full = both + other + flipped[:blocks]
        folded = jnp.where(low, full[:half_rows], full[half_rows:])
        gram_out[f] = folded
        return jnp.where(diagonal, folded, 0.0)

    def gram_copy(f):
        target = f * stride
        return pltpu.make_async_remote_copy(
            src_ref=gram_out.at[f],
            dst_ref=gram_in.at[slot_of(me, target, peers)],
            send_sem=gram_sem.at[0],
            recv_sem=gram_sem.at[1],
            device_id={"pts": target},
            device_id_type=MESH,
        )

    def opening(i, trace):
        trace = trace + pack(order(jnp.maximum(i - 1, 0)))
        local_gram(order(i))
        return trace

    trace = lax.fori_loop(0, hold, opening, jnp.zeros((half_rows, wide), f32))
    pl.semaphore_wait(barrier, peers - 1 + groups - 1)
    for i in range(hold - 1):
        gram_copy(order(i)).start()

    def middle(i, trace):
        last = order(i - 1)
        trace = trace + pack(last)
        gram_copy(last).start()
        local_gram(order(i))
        return trace

    trace = lax.fori_loop(hold, freqs, middle, trace)
    trace = trace + pack(mine)
    if stride > 1:

        @pl.when(jnp.logical_not(is_owner))
        def _():
            gram_copy(mine).start()

    trace_row = jnp.sum(trace, axis=0, keepdims=True) * scaling
    trace_out[...] = trace_row

    def trace_copy(step):
        target = lax.rem(row + step, groups)
        return pltpu.make_async_remote_copy(
            src_ref=trace_out,
            dst_ref=trace_in.at[slot_of(row, target, groups)],
            send_sem=trace_sem.at[0],
            recv_sem=trace_sem.at[1],
            device_id={"freq": target},
            device_id_type=MESH,
        )

    for step in range(1, groups):
        trace_copy(step).start()

    def msg_copy(step):
        return pltpu.make_async_remote_copy(
            src_ref=message.at[mine],
            dst_ref=message.at[mine],
            send_sem=msg_send.at[0],
            recv_sem=msg_recv.at[mine],
            device_id={"pts": partner(me, step, peers)},
            device_id_type=MESH,
        )

    def scalar_copy(step):
        target = partner(me, step, peers)
        return pltpu.make_async_remote_copy(
            src_ref=scalar_out,
            dst_ref=scalar_in.at[slot_of(me, target, peers)],
            send_sem=scalar_sem.at[0],
            recv_sem=scalar_sem.at[1],
            device_id={"pts": target},
            device_id_type=MESH,
        )

    basis_load.wait()
    scalar_out[...] = jnp.zeros_like(scalar_out)

    @pl.when(is_owner)
    def _():
        wait_bytes(gram_in.at[pl.ds(0, peers - 1)], gram_sem.at[1])
        total = gram_out[mine]
        for k in range(peers - 1):
            total = total + gram_in[k]
        total = total * (0.5 * scaling)
        swapped = pltpu.roll(total, blocks, 1)
        full = jnp.concatenate(
            [jnp.where(low, total, swapped), jnp.where(low, swapped, total)], axis=0
        )
        full = jnp.concatenate([full, full], axis=0)
        flipped = full.T
        real = full + flipped
        imag = full - flipped
        top = lax.broadcasted_iota(jnp.int32, (wide, wide), 0) < blocks
        left = lax.broadcasted_iota(jnp.int32, (wide, wide), 1) < blocks
        same = top == left
        matrix = jnp.where(same, real, jnp.where(top, -imag, imag))
        turning = jnp.where(same, imag, jnp.where(top, real, -real))
        right = jnp.concatenate([matrix, turning], axis=1)

        def rounded(x):
            return x.astype(jnp.bfloat16).astype(f32)

        right_high = rounded(right)
        right_rest = right - right_high
        right_mid = rounded(right_rest)
        right_low = rounded(right_rest - right_mid)
        right_pair = jnp.concatenate([right_high, right_mid], axis=0)

        def apply(vec):
            high = rounded(vec)
            rest = vec - high
            mid = rounded(rest)
            tail = rounded(rest - mid)
            rows = jnp.concatenate(
                [
                    jnp.concatenate([high, high], axis=1),
                    jnp.concatenate([mid, mid], axis=1),
                    jnp.concatenate([tail, jnp.zeros_like(tail)], axis=1),
                ],
                axis=0,
            )
            out = jnp.dot(rows, right_pair, preferred_element_type=f32)
            small = jnp.dot(high, right_low, preferred_element_type=f32)
            out = out[:rank] + (out[rank : 2 * rank] + (out[2 * rank :] + small))
            return out[:, :wide], out[:, wide:]

        vec = jnp.concatenate([basis_ref[0], basis_ref[1]], axis=1)
        for step in range(ITERS):
            z, turned = apply(vec)
            vec = orthonormalize(z, turned, blocks, rank if step < ITERS - 1 else rank // 2)
        message[mine] = vec
        for step in range(peers - 1, 0, -1):
            msg_copy(step).start()
        energy = jnp.sum(vec * apply(vec)[0], axis=1, keepdims=True) * (1.0 / blocks)
        which = lax.broadcasted_iota(jnp.int32, (rank, wide), 0)
        columns = lax.broadcasted_iota(jnp.int32, (rank, wide), 1)
        scalar_out[0:1] = jnp.sum(jnp.where(which == columns, energy, 0.0), axis=0, keepdims=True)

    wait_bytes(trace_in.at[pl.ds(0, groups - 1)], trace_sem.at[1])
    group_trace = trace_out[...]
    for k in range(groups - 1):
        group_trace = group_trace + trace_in[k]
    scalar_out[1:2] = group_trace
    for step in range(peers - 1, 0, -1):
        scalar_copy(step).start()

    inverse = inverse_ref[...]

    def arrive(i):
        f = partner(mine, i, freqs)
        if stride > 1:

            @pl.when(jnp.logical_or(i > 0, jnp.logical_not(is_owner)))
            def _():
                wait_bytes(message.at[f], msg_recv.at[f])
        else:

            @pl.when(i > 0)
            def _():
                wait_bytes(message.at[f], msg_recv.at[f])

        return f

    def ahead(i, carry):
        f = arrive(i)
        project_one(message[f], split, f, inverse, stage, f)
        return carry

    lax.fori_loop(0, early, ahead, 0)

    def others(i, carry):
        arrive(i)
        return carry

    lax.fori_loop(early, freqs, others, 0)
    wait_bytes(scalar_in.at[pl.ds(0, peers - 1)], scalar_sem.at[1])
    message_ref[...] = message[...]
    scalar_ref[pl.ds(0, peers - 1)] = scalar_in[pl.ds(0, peers - 1)]
    scalar_ref[peers - 1] = scalar_out[...]

    if stride > 1:

        @pl.when(jnp.logical_not(is_owner))
        def _():
            wait_bytes(gram_out, gram_sem.at[0])

        @pl.when(is_owner)
        def _():
            wait_bytes(gram_out.at[pl.ds(0, freqs - 1)], gram_sem.at[0])
    else:
        wait_bytes(gram_out.at[pl.ds(0, freqs - 1)], gram_sem.at[0])

    wait_bytes(trace_in.at[pl.ds(0, groups - 1)], trace_sem.at[0])
    wait_bytes(scalar_in.at[pl.ds(0, peers - 1)], scalar_sem.at[0])

    @pl.when(is_owner)
    def _():
        wait_bytes(gram_in.at[pl.ds(0, peers - 1), pl.ds(0, rank)], msg_send.at[0])


def project_kernel(
    count,
    freqs,
    peers,
    early,
    inverse_ref,
    split,
    message,
    scalar,
    stage,
    basis_out,
    spectrum_out,
    modes_out,
    late_stage,
    basis_stage,
    spectrum_stage,
    store_sem,
):
    wide = message.shape[2]
    blocks = wide // 2
    rank = message.shape[1]
    stride = peers // freqs
    me = lax.axis_index("pts")
    mine = lax.div(me, stride)

    def start(i, carry):
        f = partner(mine, i, freqs)
        pltpu.make_async_copy(stage.at[f], modes_out.at[:, f], store_sem.at[0]).start()
        return carry

    lax.fori_loop(0, early, start, 0)

    def late(i, carry):
        f = partner(mine, i, freqs)
        project_one(message[f], split, f, inverse_ref[...], late_stage, i - early)
        pltpu.make_async_copy(
            late_stage.at[i - early], modes_out.at[:, f], store_sem.at[0]
        ).start()
        return carry

    lax.fori_loop(early, freqs, late, 0)

    vecs = message[...]
    turned = pltpu.roll(vecs, blocks, 2)
    basis_stage[0] = vecs[:, :, :blocks]
    basis_stage[1] = turned[:, :, :blocks]
    basis_store = pltpu.make_async_copy(basis_stage, basis_out, store_sem.at[1])
    basis_store.start()

    energies = []
    for f in range(freqs):
        energies.append(scalar[slot_of(f * stride, me, peers), 0:1])
    overall = jnp.zeros((1, wide), jnp.float32)
    for k in range(peers):
        overall = overall + scalar[k, 1:2]
    overall = jnp.sum(overall, axis=1, keepdims=True)
    spectrum = jnp.concatenate(energies, axis=0) * count / overall
    spectrum_stage[...] = spectrum[:, :rank]
    spectrum_store = pltpu.make_async_copy(spectrum_stage, spectrum_out, store_sem.at[2])
    spectrum_store.start()

    wait_bytes(modes_out, store_sem.at[0])
    basis_store.wait()
    spectrum_store.wait()


def per_device(peers, groups, data, quad_weight, basis):
    _, freqs, blocks, comps, points = data.shape
    rank = basis.shape[-1]
    assert peers % freqs == 0 and freqs > 2
    scaling = 1.0 / (comps * points * peers)
    wide = 2 * blocks
    early = freqs - 2
    vmem = pl.BlockSpec(memory_space=pltpu.VMEM)
    anywhere = pl.BlockSpec(memory_space=pl.ANY)
    f32 = jnp.float32
    weight = quad_weight.reshape(1, points)
    hbm = pl.BlockSpec(memory_space=pltpu.HBM)
    in_hbm = functools.partial(pltpu.with_memory_space_constraint, memory_space=pltpu.HBM)
    split, message, scalar, inverse, stage = pl.pallas_call(
        functools.partial(spod_kernel, scaling, freqs, peers, groups, early),
        out_shape=(
            pltpu.VMEM((freqs, comps, 2 * wide, points), jnp.bfloat16),
            pltpu.VMEM((freqs, rank, wide), f32),
            pltpu.VMEM((peers, 2, wide), f32),
            pltpu.VMEM((1, points), f32),
            pltpu.VMEM((freqs, 2, comps, rank, points), f32),
        ),
        in_specs=[hbm, hbm, hbm],
        out_specs=(vmem, vmem, vmem, vmem, vmem),
        scratch_shapes=[
            pltpu.VMEM((freqs, 2, comps, blocks, points), f32),
            pltpu.VMEM((1, points), f32),
            pltpu.VMEM((2, rank, blocks), f32),
            pltpu.VMEM((wide, wide), f32),
            pltpu.VMEM((freqs, blocks // 2, wide), f32),
            pltpu.VMEM((peers, blocks // 2, wide), f32),
            pltpu.VMEM((1, wide), f32),
            pltpu.VMEM((groups, 1, wide), f32),
            pltpu.VMEM((freqs, rank, wide), f32),
            pltpu.VMEM((2, wide), f32),
            pltpu.VMEM((peers, 2, wide), f32),
            pltpu.SemaphoreType.DMA((2,)),
            pltpu.SemaphoreType.DMA((freqs,)),
            pltpu.SemaphoreType.DMA((2,)),
            pltpu.SemaphoreType.DMA((2,)),
            pltpu.SemaphoreType.DMA((1,)),
            pltpu.SemaphoreType.DMA((freqs,)),
            pltpu.SemaphoreType.DMA((2,)),
        ],
        compiler_params=pltpu.CompilerParams(
            collective_id=0, has_side_effects=True, vmem_limit_bytes=44 * 1024 * 1024
        ),
        name="spod",
    )(
        in_hbm(data.transpose(0, 1, 3, 2, 4)),
        in_hbm(weight),
        in_hbm(basis.transpose(0, 1, 3, 2)),
    )
    basis_t, spectrum, modes_t = pl.pallas_call(
        functools.partial(project_kernel, freqs * groups * blocks, freqs, peers, early),
        out_shape=(
            jax.ShapeDtypeStruct((2, freqs, rank, blocks), f32),
            jax.ShapeDtypeStruct((freqs, rank), f32),
            jax.ShapeDtypeStruct((2, freqs, comps, rank, points), f32),
        ),
        in_specs=[vmem, vmem, vmem, vmem, vmem],
        out_specs=(anywhere, anywhere, anywhere),
        scratch_shapes=[
            pltpu.VMEM((freqs - early, 2, comps, rank, points), f32),
            pltpu.VMEM((2, freqs, rank, blocks), f32),
            pltpu.VMEM((freqs, rank), f32),
            pltpu.SemaphoreType.DMA((3,)),
        ],
        compiler_params=pltpu.CompilerParams(vmem_limit_bytes=20 * 1024 * 1024),
        name="project",
    )(inverse, split, message, scalar, stage)
    return (
        basis_t.transpose(0, 1, 3, 2),
        spectrum,
        modes_t.transpose(0, 1, 3, 2, 4),
    )


def solution(mesh):
    in_specs = (P(None, "freq", None, None, "pts"), P("pts"), P(None, "freq", None, None))
    out_specs = (P(None, "freq", None, None), P("freq", None), P(None, "freq", None, None, "pts"))
    body = functools.partial(per_device, mesh.shape["pts"], mesh.shape["freq"])
    return jax.shard_map(
        body, mesh=mesh, in_specs=in_specs, out_specs=out_specs, check_vma=False
    )
```

time: 25.8 us -> 21.7 us (0.84)
  Pallas kernels: 25 us -> 20.9 us
    pallas_call x1, Pallas kernels: 21.3 us -> 19.1 us  [per_device(): pl.pallas_call(functools.partial(spod_kernel, scaling, freqs, peers, grou...]
    pallas_call x1, Pallas kernels: 3.66 us -> 1.73 us  [per_device(): pl.pallas_call(functools.partial(project_kernel, freqs * groups * blocks,...]
where the time goes in v1:
time: 21.7 us; the launch traced here: 21.5 us
  Pallas kernels  20.9 us (96%)
  between operations  0.64 us (3%)
    pallas_call x1, Pallas kernels, per_device(): pl.pallas_call(functools.partial(spod_kernel, scaling, freqs, peers, grou...  19.1 us
    pallas_call x1, Pallas kernels, per_device(): pl.pallas_call(functools.partial(project_kernel, freqs * groups * blocks,...  1.73 us

profile of v1, /device:TPU:0, one launch (start us, length us, event | category | flops | bytes accessed | tf_op | source)
XLA Modules:
  0.0 21.5 jit_solution(972445355224228438)
XLA Ops:
  0.6 19.1 %spod.1 = (bf16[8,3,256,1024]{3,2,1,0:T(8,128)(2,1)S(1)}, f32[8,8,128]{2,1,0:T(8,128)S(1)}, f32[8,2,128]{2,1,0:T(2,128)S(1)}, f32[1,1024]{1,0:T(1,128)S(1)}, f32[8,2,3,8,1024]{4,3,2,1,0:T(8,128)S(1)}) custom-call(f32[2,8,3,64,1024]{4,3,2,1,0:T(8,128)} %bitcast.5, f32[1,1024]{1,0:T(1,128)} %bitcast.7, f32[2,8,8,64]{3,2,1,0:T(8,128)} %bitcast.6), custom_call_target="tpu_custom_call" | custom-call | tf_op jit(solution)/shard_map/spod/pallas_call | solution.py:481
  19.8 1.7 %project.1 = (f32[2,8,8,64]{3,2,1,0:T(8,128)}, f32[8,8]{1,0:T(8,128)}, f32[2,8,3,8,1024]{4,3,2,1,0:T(8,128)}) custom-call(f32[1,1024]{1,0:T(1,128)S(1)} %get-tuple-element.11.inverse_ref, bf16[8,3,256,1024]{3,2,1,0:T(8,128)(2,1)S(1)} %get-tuple-element.12.split, f32[8,8,128]{2,1,0:T(8,128)S(1)} %get-tuple-element.13.message, ...), custom_call_target="tpu_custom_call" | custom-call | tf_op jit(solution)/shard_map/project/pallas_call | solution.py:521

commit v2 on v1

--- a/solution.py
+++ b/solution.py
@@ -9,6 +9,8 @@
 
 ITERS = 4
 EPS = 1e-06
+HOLD = 2
+LATE = 4
 MESH = pl.DeviceIdType.MESH
 
 
@@ -26,6 +28,26 @@
             result = result + bit * (one + other - 2 * one * other)
         bit *= 2
     return result
+
+
+def farthest_first(index, i, size):
+    if size % 2 or size & (size - 1):
+        return partner(index, size - 1 - i, size)
+    pair, core = lax.div(index, 2), lax.rem(index, 2)
+    mask, odd = (size - 1 - i) // 2, lax.rem(i, 2)
+    other = 1 - core
+    odd = jnp.where(mask == 0, jnp.where(odd == 0, other, core), odd)
+    return 2 * partner(pair, mask, size // 2) + odd
+
+
+def nearest_first(index, i, size):
+    if size % 2 or size & (size - 1) or size < 4:
+        return partner(index, i, size)
+    pair, core = lax.div(index, 2), lax.rem(index, 2)
+    pairs = size // 2
+    mask = jnp.where(i < 2, 0, 1 + lax.rem(i + pairs - 3, pairs - 1))
+    odd = jnp.where(i < 2, jnp.where(i == 0, core, 1 - core), jnp.where(i < pairs + 1, 1, 0))
+    return 2 * partner(pair, mask, pairs) + odd
 
 
 def slot_of(source, target, size):
@@ -99,10 +121,11 @@
     data_ref,
     weight_hbm,
     basis_hbm,
+    message_ref,
+    energy_ref,
+    trace_ref,
+    inverse_ref,
     split,
-    message_ref,
-    scalar_ref,
-    inverse_ref,
     stage,
     buf,
     weight_ref,
@@ -113,15 +136,16 @@
     trace_out,
     trace_in,
     message,
-    scalar_out,
-    scalar_in,
+    energy_out,
+    energy_in,
     small_sem,
     load_sem,
     gram_sem,
     trace_sem,
     msg_send,
     msg_recv,
-    scalar_sem,
+    energy_sem,
+    group_sem,
 ):
     comps, blocks, points = buf.shape[2], buf.shape[3], buf.shape[4]
     rank = basis_ref.shape[1]
@@ -132,14 +156,19 @@
     row = lax.axis_index("freq")
     mine = lax.div(me, stride)
     is_owner = lax.rem(me, stride) == 0
-    hold = min(2, freqs - 1)
+    everyone = groups * peers
+    hold = min(HOLD, freqs - 1)
     f32 = jnp.float32
 
     def load(f):
         return pltpu.make_async_copy(data_ref.at[:, f], buf.at[f], load_sem.at[f])
 
+    def anyone(step):
+        across, along = step // peers, step % peers
+        return {"freq": partner(row, across, groups), "pts": partner(me, along, peers)}
+
     def order(i):
-        return partner(mine, freqs - 1 - i, freqs)
+        return farthest_first(mine, i, freqs)
 
     weight_load = pltpu.make_async_copy(weight_hbm, weight_ref, small_sem.at[0])
     basis_load = pltpu.make_async_copy(basis_hbm.at[:, mine], basis_ref, small_sem.at[1])
@@ -151,11 +180,11 @@
     barrier = pltpu.get_barrier_semaphore()
     for step in range(1, peers):
         pl.semaphore_signal(
-            barrier, inc=1, device_id={"pts": lax.rem(me + step, peers)}, device_id_type=MESH
+            barrier, inc=1, device_id={"pts": partner(me, step, peers)}, device_id_type=MESH
         )
     for step in range(1, groups):
         pl.semaphore_signal(
-            barrier, inc=1, device_id={"freq": lax.rem(row + step, groups)}, device_id_type=MESH
+            barrier, inc=1, device_id={"freq": partner(row, step, groups)}, device_id_type=MESH
         )
 
     lanes = lax.broadcasted_iota(jnp.int32, (1, wide), 1)
@@ -164,15 +193,14 @@
     raw[...] = jnp.zeros_like(raw)
     weight_load.wait()
     root = jnp.sqrt(weight_ref[...])
-    inverse_ref[...] = (1.0 / blocks) / root
+    inverse = (1.0 / blocks) / root
+    inverse_ref[...] = inverse
 
     rows_at = lax.broadcasted_iota(jnp.int32, (half_rows, wide), 0)
     cols_at = lax.broadcasted_iota(jnp.int32, (half_rows, wide), 1)
     diagonal = jnp.logical_or(cols_at == rows_at, cols_at == rows_at + blocks + half_rows)
 
     def local_gram(f):
-        load(f).wait()
-        total = jnp.zeros((2 * wide, wide), f32)
         for c in range(comps):
             for part in range(2):
                 value = buf[f, part, c] * root
@@ -180,6 +208,8 @@
                 rest = (value - high.astype(f32)).astype(jnp.bfloat16)
                 split[f, c, part * blocks : (part + 1) * blocks] = high
                 split[f, c, wide + part * blocks : wide + (part + 1) * blocks] = rest
+        total = jnp.zeros((2 * wide, wide), f32)
+        for c in range(comps):
             total = total + lax.dot_general(
                 split[f, c],
                 split[f, c, :wide],
@@ -211,20 +241,26 @@
         )
 
     def opening(i, trace):
+        load(order(i)).wait()
         trace = trace + pack(order(jnp.maximum(i - 1, 0)))
         local_gram(order(i))
         return trace
 
     trace = lax.fori_loop(0, hold, opening, jnp.zeros((half_rows, wide), f32))
     pl.semaphore_wait(barrier, peers - 1 + groups - 1)
+    for step in range(1, groups):
+        pl.semaphore_signal(
+            group_sem, inc=1, device_id={"freq": partner(row, step, groups)}, device_id_type=MESH
+        )
     for i in range(hold - 1):
         gram_copy(order(i)).start()
 
     def middle(i, trace):
         last = order(i - 1)
+        load(order(i)).wait()
         trace = trace + pack(last)
+        local_gram(order(i))
         gram_copy(last).start()
-        local_gram(order(i))
         return trace
 
     trace = lax.fori_loop(hold, freqs, middle, trace)
@@ -239,17 +275,19 @@
     trace_out[...] = trace_row
 
     def trace_copy(step):
-        target = lax.rem(row + step, groups)
+        target = anyone(step)
+        slot = slot_of(row * peers + me, target["freq"] * peers + target["pts"], everyone)
         return pltpu.make_async_remote_copy(
             src_ref=trace_out,
-            dst_ref=trace_in.at[slot_of(row, target, groups)],
+            dst_ref=trace_in.at[slot],
             send_sem=trace_sem.at[0],
             recv_sem=trace_sem.at[1],
-            device_id={"freq": target},
+            device_id=target,
             device_id_type=MESH,
         )
 
-    for step in range(1, groups):
+    pl.semaphore_wait(group_sem, groups - 1)
+    for step in range(everyone - 1, 0, -1):
         trace_copy(step).start()
 
     def msg_copy(step):
@@ -262,19 +300,18 @@
             device_id_type=MESH,
         )
 
-    def scalar_copy(step):
+    def energy_copy(step):
         target = partner(me, step, peers)
         return pltpu.make_async_remote_copy(
-            src_ref=scalar_out,
-            dst_ref=scalar_in.at[slot_of(me, target, peers)],
-            send_sem=scalar_sem.at[0],
-            recv_sem=scalar_sem.at[1],
+            src_ref=energy_out,
+            dst_ref=energy_in.at[slot_of(mine, lax.div(target, stride), freqs)],
+            send_sem=energy_sem.at[0],
+            recv_sem=energy_sem.at[1],
             device_id={"pts": target},
             device_id_type=MESH,
         )
 
     basis_load.wait()
-    scalar_out[...] = jnp.zeros_like(scalar_out)
 
     @pl.when(is_owner)
     def _():
@@ -335,20 +372,12 @@
         energy = jnp.sum(vec * apply(vec)[0], axis=1, keepdims=True) * (1.0 / blocks)
         which = lax.broadcasted_iota(jnp.int32, (rank, wide), 0)
         columns = lax.broadcasted_iota(jnp.int32, (rank, wide), 1)
-        scalar_out[0:1] = jnp.sum(jnp.where(which == columns, energy, 0.0), axis=0, keepdims=True)
-
-    wait_bytes(trace_in.at[pl.ds(0, groups - 1)], trace_sem.at[1])
-    group_trace = trace_out[...]
-    for k in range(groups - 1):
-        group_trace = group_trace + trace_in[k]
-    scalar_out[1:2] = group_trace
-    for step in range(peers - 1, 0, -1):
-        scalar_copy(step).start()
-
-    inverse = inverse_ref[...]
+        energy_out[...] = jnp.sum(jnp.where(which == columns, energy, 0.0), axis=0, keepdims=True)
+        for step in range(peers - 1, 0, -1):
+            energy_copy(step).start()
 
     def arrive(i):
-        f = partner(mine, i, freqs)
+        f = nearest_first(mine, i, freqs)
         if stride > 1:
 
             @pl.when(jnp.logical_or(i > 0, jnp.logical_not(is_owner)))
@@ -368,16 +397,25 @@
         return carry
 
     lax.fori_loop(0, early, ahead, 0)
-
-    def others(i, carry):
+    for i in range(early, freqs):
         arrive(i)
-        return carry
-
-    lax.fori_loop(early, freqs, others, 0)
-    wait_bytes(scalar_in.at[pl.ds(0, peers - 1)], scalar_sem.at[1])
+    wait_bytes(trace_in.at[pl.ds(0, everyone - 1)], trace_sem.at[1])
+    trace_ref[pl.ds(0, everyone - 1)] = trace_in[pl.ds(0, everyone - 1)]
+    trace_ref[everyone - 1] = trace_out[...]
+    if stride > 1:
+
+        @pl.when(jnp.logical_not(is_owner))
+        def _():
+            wait_bytes(energy_in, energy_sem.at[1])
+            energy_ref[...] = energy_in[...]
+
+    @pl.when(is_owner)
+    def _():
+        wait_bytes(energy_in.at[pl.ds(0, freqs - 1)], energy_sem.at[1])
+        energy_ref[pl.ds(0, freqs - 1)] = energy_in[pl.ds(0, freqs - 1)]
+        energy_ref[freqs - 1] = energy_out[...]
+
     message_ref[...] = message[...]
-    scalar_ref[pl.ds(0, peers - 1)] = scalar_in[pl.ds(0, peers - 1)]
-    scalar_ref[peers - 1] = scalar_out[...]
 
     if stride > 1:
 
@@ -391,23 +429,23 @@
     else:
         wait_bytes(gram_out.at[pl.ds(0, freqs - 1)], gram_sem.at[0])
 
-    wait_bytes(trace_in.at[pl.ds(0, groups - 1)], trace_sem.at[0])
-    wait_bytes(scalar_in.at[pl.ds(0, peers - 1)], scalar_sem.at[0])
+    wait_bytes(trace_in.at[pl.ds(0, everyone - 1)], trace_sem.at[0])
 
     @pl.when(is_owner)
     def _():
+        wait_bytes(trace_in.at[pl.ds(0, peers - 1)], energy_sem.at[0])
         wait_bytes(gram_in.at[pl.ds(0, peers - 1), pl.ds(0, rank)], msg_send.at[0])
 
 
-def project_kernel(
+def store_kernel(
     count,
-    freqs,
     peers,
     early,
+    message,
+    energy,
+    trace,
     inverse_ref,
     split,
-    message,
-    scalar,
     stage,
     basis_out,
     spectrum_out,
@@ -417,29 +455,19 @@
     spectrum_stage,
     store_sem,
 ):
-    wide = message.shape[2]
+    freqs, rank, wide = message.shape
     blocks = wide // 2
-    rank = message.shape[1]
-    stride = peers // freqs
-    me = lax.axis_index("pts")
-    mine = lax.div(me, stride)
-
-    def start(i, carry):
-        f = partner(mine, i, freqs)
+    mine = lax.div(lax.axis_index("pts"), peers // freqs)
+
+    for i in range(early):
+        f = nearest_first(mine, i, freqs)
         pltpu.make_async_copy(stage.at[f], modes_out.at[:, f], store_sem.at[0]).start()
-        return carry
-
-    lax.fori_loop(0, early, start, 0)
-
-    def late(i, carry):
-        f = partner(mine, i, freqs)
+    for i in range(early, freqs):
+        f = nearest_first(mine, i, freqs)
         project_one(message[f], split, f, inverse_ref[...], late_stage, i - early)
         pltpu.make_async_copy(
             late_stage.at[i - early], modes_out.at[:, f], store_sem.at[0]
         ).start()
-        return carry
-
-    lax.fori_loop(early, freqs, late, 0)
 
     vecs = message[...]
     turned = pltpu.roll(vecs, blocks, 2)
@@ -448,14 +476,11 @@
     basis_store = pltpu.make_async_copy(basis_stage, basis_out, store_sem.at[1])
     basis_store.start()
 
-    energies = []
-    for f in range(freqs):
-        energies.append(scalar[slot_of(f * stride, me, peers), 0:1])
-    overall = jnp.zeros((1, wide), jnp.float32)
-    for k in range(peers):
-        overall = overall + scalar[k, 1:2]
-    overall = jnp.sum(overall, axis=1, keepdims=True)
-    spectrum = jnp.concatenate(energies, axis=0) * count / overall
+    energies = jnp.concatenate(
+        [energy[slot_of(f, mine, freqs)] for f in range(freqs)], axis=0
+    )
+    overall = jnp.sum(jnp.sum(trace[...], axis=0), axis=1, keepdims=True)
+    spectrum = energies * count / overall
     spectrum_stage[...] = spectrum[:, :rank]
     spectrum_store = pltpu.make_async_copy(spectrum_stage, spectrum_out, store_sem.at[2])
     spectrum_store.start()
@@ -471,24 +496,26 @@
     assert peers % freqs == 0 and freqs > 2
     scaling = 1.0 / (comps * points * peers)
     wide = 2 * blocks
-    early = freqs - 2
+    everyone = groups * peers
+    early = freqs - LATE
     vmem = pl.BlockSpec(memory_space=pltpu.VMEM)
     anywhere = pl.BlockSpec(memory_space=pl.ANY)
     f32 = jnp.float32
     weight = quad_weight.reshape(1, points)
     hbm = pl.BlockSpec(memory_space=pltpu.HBM)
     in_hbm = functools.partial(pltpu.with_memory_space_constraint, memory_space=pltpu.HBM)
-    split, message, scalar, inverse, stage = pl.pallas_call(
+    message, energy, trace, inverse, split, stage = pl.pallas_call(
         functools.partial(spod_kernel, scaling, freqs, peers, groups, early),
         out_shape=(
+            pltpu.VMEM((freqs, rank, wide), f32),
+            pltpu.VMEM((freqs, 1, wide), f32),
+            pltpu.VMEM((everyone, 1, wide), f32),
+            pltpu.VMEM((1, points), f32),
             pltpu.VMEM((freqs, comps, 2 * wide, points), jnp.bfloat16),
-            pltpu.VMEM((freqs, rank, wide), f32),
-            pltpu.VMEM((peers, 2, wide), f32),
-            pltpu.VMEM((1, points), f32),
             pltpu.VMEM((freqs, 2, comps, rank, points), f32),
         ),
         in_specs=[hbm, hbm, hbm],
-        out_specs=(vmem, vmem, vmem, vmem, vmem),
+        out_specs=(vmem, vmem, vmem, vmem, vmem, vmem),
         scratch_shapes=[
             pltpu.VMEM((freqs, 2, comps, blocks, points), f32),
             pltpu.VMEM((1, points), f32),
@@ -497,10 +524,10 @@
             pltpu.VMEM((freqs, blocks // 2, wide), f32),
             pltpu.VMEM((peers, blocks // 2, wide), f32),
             pltpu.VMEM((1, wide), f32),
-            pltpu.VMEM((groups, 1, wide), f32),
+            pltpu.VMEM((everyone, 1, wide), f32),
             pltpu.VMEM((freqs, rank, wide), f32),
-            pltpu.VMEM((2, wide), f32),
-            pltpu.VMEM((peers, 2, wide), f32),
+            pltpu.VMEM((1, wide), f32),
+            pltpu.VMEM((freqs, 1, wide), f32),
             pltpu.SemaphoreType.DMA((2,)),
             pltpu.SemaphoreType.DMA((freqs,)),
             pltpu.SemaphoreType.DMA((2,)),
@@ -508,6 +535,7 @@
             pltpu.SemaphoreType.DMA((1,)),
             pltpu.SemaphoreType.DMA((freqs,)),
             pltpu.SemaphoreType.DMA((2,)),
+            pltpu.SemaphoreType.REGULAR,
         ],
         compiler_params=pltpu.CompilerParams(
             collective_id=0, has_side_effects=True, vmem_limit_bytes=44 * 1024 * 1024
@@ -519,13 +547,13 @@
         in_hbm(basis.transpose(0, 1, 3, 2)),
     )
     basis_t, spectrum, modes_t = pl.pallas_call(
-        functools.partial(project_kernel, freqs * groups * blocks, freqs, peers, early),
+        functools.partial(store_kernel, freqs * groups * blocks, peers, early),
         out_shape=(
             jax.ShapeDtypeStruct((2, freqs, rank, blocks), f32),
             jax.ShapeDtypeStruct((freqs, rank), f32),
             jax.ShapeDtypeStruct((2, freqs, comps, rank, points), f32),
         ),
-        in_specs=[vmem, vmem, vmem, vmem, vmem],
+        in_specs=[vmem, vmem, vmem, vmem, vmem, vmem],
         out_specs=(anywhere, anywhere, anywhere),
         scratch_shapes=[
             pltpu.VMEM((freqs - early, 2, comps, rank, points), f32),
@@ -534,8 +562,8 @@
             pltpu.SemaphoreType.DMA((3,)),
         ],
         compiler_params=pltpu.CompilerParams(vmem_limit_bytes=20 * 1024 * 1024),
-        name="project",
-    )(inverse, split, message, scalar, stage)
+        name="store",
+    )(message, energy, trace, inverse, split, stage)
     return (
         basis_t.transpose(0, 1, 3, 2),
         spectrum,

time: 21.7 us -> 20 us (0.922)
  Pallas kernels: 20.9 us -> 19.2 us
    pallas_call x1, Pallas kernels: 19.1 us -> 17.2 us  [per_device(): pl.pallas_call(functools.partial(spod_kernel, scaling, freqs, peers, grou...]
    pallas_call x1, Pallas kernels: 1.73 us -> 1.96 us  [per_device(): pl.pallas_call(functools.partial(store_kernel, freqs * groups * blocks, p...]
where the time goes in v2:
time: 20 us; the launch traced here: 19.8 us
  Pallas kernels  19.2 us (96%)
  between operations  0.64 us (3%)
    pallas_call x1, Pallas kernels, per_device(): pl.pallas_call(functools.partial(spod_kernel, scaling, freqs, peers, grou...  17.2 us
    pallas_call x1, Pallas kernels, per_device(): pl.pallas_call(functools.partial(store_kernel, freqs * groups * blocks, p...  1.96 us

profile of v2, /device:TPU:0, one launch (start us, length us, event | category | flops | bytes accessed | tf_op | source)
XLA Modules:
  0.0 19.8 jit_solution(17905641218847065186)
XLA Ops:
  0.6 17.2 %spod.1 = (f32[8,8,128]{2,1,0:T(8,128)S(1)}, f32[8,1,128]{2,1,0:T(1,128)S(1)}, f32[32,1,128]{2,1,0:T(1,128)S(1)}, f32[1,1024]{1,0:T(1,128)S(1)}, bf16[8,3,256,10...) custom-call(f32[2,8,3,64,1024]{4,3,2,1,0:T(8,128)} %bitcast.5, f32[1,1024]{1,0:T(1,128)} %bitcast.7, ...), custom_call_target="tpu_custom_call" | custom-call | tf_op jit(solution)/shard_map/spod/pallas_call | solution.py:507
  17.8 2.0 %store.1 = (f32[2,8,8,64]{3,2,1,0:T(8,128)}, f32[8,8]{1,0:T(8,128)}, f32[2,8,3,8,1024]{4,3,2,1,0:T(8,128)}) custom-call(f32[8,8,128]{2,1,0:T(8,128)S(1)} %get-tuple-element.12.message, f32[8,1,128]{2,1,0:T(1,128)S(1)} %get-tuple-element.13.energy, f32[32,1,128]{2,1,0:T(1,128)S(1)} %get-tuple-element.14.trace, f32[1,1024]{1,0:T(1,128)S(1)} %get-tuple-element.15.inverse_ref, ...), custom_call_target="tpu_custom_call" | custom-call | tf_op jit(solution)/shard_map/store/pallas_call | solution.py:549

commit v3 on v2

--- a/solution.py
+++ b/solution.py
@@ -10,7 +10,7 @@
 ITERS = 4
 EPS = 1e-06
 HOLD = 2
-LATE = 4
+LATE = 2
 MESH = pl.DeviceIdType.MESH
 
 
@@ -41,13 +41,12 @@
 
 
 def nearest_first(index, i, size):
-    if size % 2 or size & (size - 1) or size < 4:
+    if size % 2 or size & (size - 1):
         return partner(index, i, size)
     pair, core = lax.div(index, 2), lax.rem(index, 2)
-    pairs = size // 2
-    mask = jnp.where(i < 2, 0, 1 + lax.rem(i + pairs - 3, pairs - 1))
-    odd = jnp.where(i < 2, jnp.where(i == 0, core, 1 - core), jnp.where(i < pairs + 1, 1, 0))
-    return 2 * partner(pair, mask, pairs) + odd
+    mask, even = i // 2 if isinstance(i, int) else lax.div(i, 2), lax.rem(i, 2)
+    odd = jnp.where(mask == 0, jnp.where(even == 0, core, 1 - core), 1 - even)
+    return 2 * partner(pair, mask, size // 2) + odd
 
 
 def slot_of(source, target, size):
@@ -98,10 +97,9 @@
             across = jnp.where(later, imag[j], 0.0)
             for k in rows:
                 if k > j:
-                    up = along[k : k + 1] * gain
-                    side = across[k : k + 1] * gain
-                    real[k] = real[k] - (up * along + side * across)
-                    imag[k] = imag[k] - (up * across - side * along)
+                    up, side = along[k : k + 1], across[k : k + 1]
+                    real[k] = real[k] - gain * (up * along + side * across)
+                    imag[k] = imag[k] - gain * (up * across - side * along)
             unit = z[j : j + 1] * factor
             unit_turned = turned[j : j + 1] * factor
             along = along * factor
@@ -164,7 +162,7 @@
         return pltpu.make_async_copy(data_ref.at[:, f], buf.at[f], load_sem.at[f])
 
     def anyone(step):
-        across, along = step // peers, step % peers
+        across, along = lax.div(step, peers), lax.rem(step, peers)
         return {"freq": partner(row, across, groups), "pts": partner(me, along, peers)}
 
     def order(i):
@@ -287,8 +285,11 @@
         )
 
     pl.semaphore_wait(group_sem, groups - 1)
-    for step in range(everyone - 1, 0, -1):
-        trace_copy(step).start()
+    def tell(step, carry):
+        trace_copy(everyone - step).start()
+        return carry
+
+    lax.fori_loop(1, everyone, tell, 0)
 
     def msg_copy(step):
         return pltpu.make_async_remote_copy(
@@ -373,8 +374,12 @@
         which = lax.broadcasted_iota(jnp.int32, (rank, wide), 0)
         columns = lax.broadcasted_iota(jnp.int32, (rank, wide), 1)
         energy_out[...] = jnp.sum(jnp.where(which == columns, energy, 0.0), axis=0, keepdims=True)
-        for step in range(peers - 1, 0, -1):
-            energy_copy(step).start()
+
+        def tell_energy(step, carry):
+            energy_copy(peers - step).start()
+            return carry
+
+        lax.fori_loop(1, peers, tell_energy, 0)
 
     def arrive(i):
         f = nearest_first(mine, i, freqs)
@@ -391,12 +396,16 @@
 
         return f
 
-    def ahead(i, carry):
-        f = arrive(i)
+    def ahead(k, carry):
+        fs = [arrive(2 * k), arrive(2 * k + 1)]
+        for f in fs:
+            project_one(message[f], split, f, inverse, stage, f)
+        return carry
+
+    lax.fori_loop(0, early // 2, ahead, 0)
+    if early % 2:
+        f = arrive(early - 1)
         project_one(message[f], split, f, inverse, stage, f)
-        return carry
-
-    lax.fori_loop(0, early, ahead, 0)
     for i in range(early, freqs):
         arrive(i)
     wait_bytes(trace_in.at[pl.ds(0, everyone - 1)], trace_sem.at[1])

time: 20 us -> 19.4 us (0.970)
  Pallas kernels: 19.2 us -> 18.6 us
    pallas_call x1, Pallas kernels: 1.96 us -> 1.42 us  [per_device(): pl.pallas_call(functools.partial(store_kernel, freqs * groups * blocks, p...]
where the time goes in v3:
time: 19.4 us; the launch traced here: 19.2 us
  Pallas kernels  18.6 us (96%)
  between operations  0.64 us (3%)
    pallas_call x1, Pallas kernels, per_device(): pl.pallas_call(functools.partial(spod_kernel, scaling, freqs, peers, grou...  17.1 us
    pallas_call x1, Pallas kernels, per_device(): pl.pallas_call(functools.partial(store_kernel, freqs * groups * blocks, p...  1.42 us

profile of v3, /device:TPU:0, one launch (start us, length us, event | category | flops | bytes accessed | tf_op | source)
XLA Modules:
  0.0 19.2 jit_solution(17702336126467173054)
XLA Ops:
  0.6 17.1 %spod.1 = (f32[8,8,128]{2,1,0:T(8,128)S(1)}, f32[8,1,128]{2,1,0:T(1,128)S(1)}, f32[32,1,128]{2,1,0:T(1,128)S(1)}, f32[1,1024]{1,0:T(1,128)S(1)}, bf16[8,3,256,10...) custom-call(f32[2,8,3,64,1024]{4,3,2,1,0:T(8,128)} %bitcast.5, f32[1,1024]{1,0:T(1,128)} %bitcast.7, ...), custom_call_target="tpu_custom_call" | custom-call | tf_op jit(solution)/shard_map/spod/pallas_call | solution.py:516
  17.8 1.4 %store.1 = (f32[2,8,8,64]{3,2,1,0:T(8,128)}, f32[8,8]{1,0:T(8,128)}, f32[2,8,3,8,1024]{4,3,2,1,0:T(8,128)}) custom-call(f32[8,8,128]{2,1,0:T(8,128)S(1)} %get-tuple-element.12.message, f32[8,1,128]{2,1,0:T(1,128)S(1)} %get-tuple-element.13.energy, f32[32,1,128]{2,1,0:T(1,128)S(1)} %get-tuple-element.14.trace, f32[1,1024]{1,0:T(1,128)S(1)} %get-tuple-element.15.inverse_ref, ...), custom_call_target="tpu_custom_call" | custom-call | tf_op jit(solution)/shard_map/store/pallas_call | solution.py:558

commit v4 on v3

--- a/solution.py
+++ b/solution.py
@@ -198,6 +198,9 @@
     cols_at = lax.broadcasted_iota(jnp.int32, (half_rows, wide), 1)
     diagonal = jnp.logical_or(cols_at == rows_at, cols_at == rows_at + blocks + half_rows)
 
+    def times(left, right):
+        return lax.dot_general(left, right, (((1,), (1,)), ((), ())), preferred_element_type=f32)
+
     def local_gram(f):
         for c in range(comps):
             for part in range(2):
@@ -206,15 +209,17 @@
                 rest = (value - high.astype(f32)).astype(jnp.bfloat16)
                 split[f, c, part * blocks : (part + 1) * blocks] = high
                 split[f, c, wide + part * blocks : wide + (part + 1) * blocks] = rest
-        total = jnp.zeros((2 * wide, wide), f32)
-        for c in range(comps):
-            total = total + lax.dot_general(
-                split[f, c],
-                split[f, c, :wide],
-                (((1,), (1,)), ((), ())),
-                preferred_element_type=f32,
-            )
-        raw[...] = 0.5 * total[:wide] + total[wide:]
+        tall = jnp.zeros((2 * wide, wide), f32)
+        broad = jnp.zeros((wide, 2 * wide), f32)
+        chunk = points // 2
+        for k in range(2 * comps):
+            at = pl.ds((k % 2) * chunk, chunk)
+            whole, high = split[f, k // 2, :, at], split[f, k // 2, :wide, at]
+            if k in (0, 1, 4):
+                tall = tall + times(whole, high)
+            else:
+                broad = broad + times(high, whole)
+        raw[...] = 0.5 * (tall[:wide] + broad[:, :wide]) + (tall[wide:] + broad[:, wide:])
 
     def pack(f):
         total = raw[...]

time: 19.4 us -> 19.4 us (level)
  no operation moved by 1% of the time
where the time goes in v4:
time: 19.4 us; the launch traced here: 19.2 us
  Pallas kernels  18.5 us (95%)
  between operations  0.64 us (3%)
    pallas_call x1, Pallas kernels, per_device(): pl.pallas_call(functools.partial(spod_kernel, scaling, freqs, peers, grou...  17.1 us
    pallas_call x1, Pallas kernels, per_device(): pl.pallas_call(functools.partial(store_kernel, freqs * groups * blocks, p...  1.42 us

profile of v4, /device:TPU:0, one launch (start us, length us, event | category | flops | bytes accessed | tf_op | source)
XLA Modules:
  0.0 19.2 jit_solution(3143093731930860564)
XLA Ops:
  0.6 17.1 %spod.1 = (f32[8,8,128]{2,1,0:T(8,128)S(1)}, f32[8,1,128]{2,1,0:T(1,128)S(1)}, f32[32,1,128]{2,1,0:T(1,128)S(1)}, f32[1,1024]{1,0:T(1,128)S(1)}, bf16[8,3,256,10...) custom-call(f32[2,8,3,64,1024]{4,3,2,1,0:T(8,128)} %bitcast.5, f32[1,1024]{1,0:T(1,128)} %bitcast.7, ...), custom_call_target="tpu_custom_call" | custom-call | tf_op jit(solution)/shard_map/spod/pallas_call | solution.py:521
  17.7 1.4 %store.1 = (f32[2,8,8,64]{3,2,1,0:T(8,128)}, f32[8,8]{1,0:T(8,128)}, f32[2,8,3,8,1024]{4,3,2,1,0:T(8,128)}) custom-call(f32[8,8,128]{2,1,0:T(8,128)S(1)} %get-tuple-element.12.message, f32[8,1,128]{2,1,0:T(1,128)S(1)} %get-tuple-element.13.energy, f32[32,1,128]{2,1,0:T(1,128)S(1)} %get-tuple-element.14.trace, f32[1,1024]{1,0:T(1,128)S(1)} %get-tuple-element.15.inverse_ref, ...), custom_call_target="tpu_custom_call" | custom-call | tf_op jit(solution)/shard_map/store/pallas_call | solution.py:563
